TPU v7x, 512 devices: a whole 4x8x8 slice. The times are simulated.
512 devices in a mesh: dp: 64 (over z_hi, x, y), expert: 8 (over z_lo, core).
Axes of the slice: x: 4, y: 8, z: 8 (z_hi: 2, z_lo: 4; z = z_hi * 4 + z_lo), core: 2. Of those that a mesh axis runs over, the one named last changes fastest.
Arguments:
- tokens: bfloat16 [65536, 3072], P('dp'), may hold values from -16 to 16
- hidden_grads: bfloat16 [65536, 1024], P('dp', 'expert'), may hold values from -6 to 6
- routed: int32 [64], P('dp'), may hold values from 1 to 1024, 49152 in all
- master: float32 [2, 8192, 3072], P(None, 'expert', 'dp'), may hold values from -6 to 6
- moment_one: float32 [2, 1024, 3072], P(None, 'expert', 'dp'), may hold values from -3 to 3
- moment_two: float32 [2, 1024, 3072], P(None, 'expert', 'dp'), may hold values from 0.05 to 1
- hot_units: int32 [1024], P('expert'), may hold values from 0 to 1023, as said below
- cold_blocks: float32 [2, 8192, 3072], P(None, 'expert', 'dp'), may hold values from -6 to 6
- cold_shift: int32 [8192], P('expert'), may hold values from 0 to 7, as said below
Outputs:
- new_master: float32 [2, 8192, 3072], P(None, 'expert', 'dp')
- new_moment_one: float32 [2, 1024, 3072], P(None, 'expert', 'dp')
- new_moment_two: float32 [2, 1024, 3072], P(None, 'expert', 'dp')
Inputs may be any that keep to these rules, and one draw needn't show every extreme that they name: `routed`: the counts sum to 49152 and one of them equals 1024. `hot_units`: within each aligned block of 128 entries the values are distinct. `cold_shift`: within each aligned block of 1024 entries every value occurs exactly 8192 // 8 // 8 times.
All inputs are finite; a program needn't handle non-finite values. No bound on the sum of `routed` on one device may be relied on, other than what follows from the above.
Results may differ from a plain program's by a relative error of at most 0.003.
Values may be sent and summed in bfloat16 or wider, within the bound.
A program may use at most 64 MiB of HBM per device.

v0:
```python
import jax
import jax.numpy as jnp
from jax import lax
from jax.sharding import Mesh
from jax.sharding import PartitionSpec as P

D = 3072
DP = ("dp_0", "dp_1", "dp_2")
beta_one = 0.9
beta_two = 0.95
step_rate = 0.1
adam_eps = 1e-08


def joined_along(tiles, dim):
    tiles = jnp.moveaxis(tiles, 0, dim)
    shape = tiles.shape
    return tiles.reshape(*shape[:dim], shape[dim] * shape[dim + 1], *shape[dim + 2 :])


def sent_to_all(value, axis):
    copies = jnp.broadcast_to(value, (lax.axis_size(axis), *value.shape))
    return lax.all_to_all(copies, axis, split_axis=0, concat_axis=0, tiled=True)


def collect(value, axis, dim):
    return joined_along(sent_to_all(value, axis), dim)


def stacked_from(value, axes, order):
    tiles = value[None]
    for k in order:
        tiles = lax.all_gather(tiles, axes[k], axis=0, tiled=True)
    block = [lax.axis_size(axes[k]) for k in reversed(order)]
    tiles = tiles.reshape(*block, *value.shape)
    turned = sorted(range(len(order)), key=lambda place: order[len(order) - 1 - place])
    return tiles.transpose(*turned, *range(len(order), tiles.ndim)).reshape(-1, *value.shape)


def gather_axes(value, axes, order, dim):
    return joined_along(stacked_from(value, axes, order), dim)


def cut_along(value, dim, peers):
    before, after = (value.shape[:dim], value.shape[dim + 1 :])
    return jnp.moveaxis(value.reshape(*before, peers, -1, *after), dim, 0)


def sum_at_owner(value, axis, dim):
    tiles = cut_along(value, dim, lax.axis_size(axis))
    arrived = lax.all_to_all(tiles, axis, split_axis=0, concat_axis=0, tiled=True)
    return arrived.sum(axis=0)


def sum_in_two_steps(value, axes, dim):
    far, near = axes
    own = sum_at_owner(cut_along(value, dim, lax.axis_size(far)), near, dim + 1)
    return jnp.sum(lax.all_to_all(own, far, 0, 0, tiled=True), axis=0)


def contract_last(left, right):
    return lax.dot_general(
        left, right, (((1,), (1,)), ((), ())), preferred_element_type=jnp.float32
    )


def contract_first(left, right):
    return lax.dot_general(
        left, right, (((0,), (0,)), ((), ())), preferred_element_type=jnp.float32
    )


def rows_with(shift_row, wanted, capacity):
    span = shift_row.shape[0]
    places = jnp.arange(span, dtype=jnp.int32)
    sort_key = jnp.where(shift_row == wanted, places, places + span)
    return jnp.argsort(sort_key, stable=True)[:capacity]


def return_cold(cold_blocks, cold_shift):
    cycle_size = lax.axis_size("expert")
    span = cold_shift.shape[0]
    capacity = span // cycle_size
    cycle_index = lax.axis_index("expert")
    owner_shift = collect(cold_shift, "expert", 0).reshape(cycle_size, span)
    places = jnp.arange(cycle_size, dtype=jnp.int32)
    send_rows = jax.vmap(lambda row, wanted: rows_with(row, wanted, capacity))(
        owner_shift, (places - cycle_index) % cycle_size
    )
    packed = cold_blocks[:, send_rows.reshape(-1), :].reshape(
        2, cycle_size, capacity, cold_blocks.shape[2]
    )
    arrived = lax.all_to_all(packed, "expert", split_axis=1, concat_axis=1, tiled=True)
    take_rows = jax.vmap(lambda wanted: rows_with(cold_shift, wanted, capacity))(
        (cycle_index - places) % cycle_size
    )
    received = (
        jnp.zeros_like(cold_blocks)
        .at[:, take_rows.reshape(-1), :]
        .set(arrived.reshape(2, cycle_size * capacity, cold_blocks.shape[2]))
    )
    return received


def per_device(
    tokens, hidden_grads, routed, master, moment_one, moment_two, hot_units, cold_blocks, cold_shift
):
    weight_scale = D ** (-0.5)
    tok_count = tokens.shape[0]
    master_hot = master[:, hot_units, :]
    weights = master_hot.astype(jnp.bfloat16)
    weight_piece = gather_axes(weights, DP, (0, 1, 2), 2)
    gate_sum = contract_last(tokens, weight_piece[0])
    up_sum = contract_last(tokens, weight_piece[1])
    gate_pre = gate_sum * weight_scale
    up_pre = up_sum * weight_scale
    live_rows = (jnp.arange(tok_count, dtype=jnp.int32) < routed[0]).astype(jnp.float32)[:, None]
    cotangent = hidden_grads.astype(jnp.float32)
    sigmoid = jax.nn.sigmoid(gate_pre)
    d_up = (live_rows * cotangent * gate_pre * sigmoid).astype(jnp.bfloat16)
    d_gate = (live_rows * cotangent * up_pre * sigmoid * (1.0 + gate_pre * (1.0 - sigmoid))).astype(
        jnp.bfloat16
    )
    partial_value = (
        jnp.stack([contract_first(d_gate, tokens), contract_first(d_up, tokens)]) * weight_scale
    )
    grad_shard = sum_in_two_steps(partial_value, ("dp_0", ("dp_1", "dp_2")), 2)
    first_new = beta_one * moment_one + (1.0 - beta_one) * grad_shard
    second_new = beta_two * moment_two + (1.0 - beta_two) * grad_shard * grad_shard
    adam = master_hot - step_rate * first_new / (jnp.sqrt(second_new) + adam_eps)
    received = return_cold(cold_blocks, cold_shift)
    new_master = received.at[:, hot_units, :].set(adam)
    return (new_master, first_new, second_new)


def solution(mesh):
    finer = Mesh(
        mesh.devices.reshape(2, 4, 8, mesh.shape["expert"]), ("dp_0", "dp_1", "dp_2", "expert")
    )
    placed = (
        P(DP, None),
        P(DP, "expert"),
        P(DP),
        P(None, "expert", DP),
        P(None, "expert", DP),
        P(None, "expert", DP),
        P("expert"),
        P(None, "expert", DP),
        P("expert"),
    )
    return jax.shard_map(
        per_device,
        mesh=finer,
        in_specs=placed,
        out_specs=(P(None, "expert", DP), P(None, "expert", DP), P(None, "expert", DP)),
        check_vma=False,
    )
```

profile of v0, /device:TPU:1, one launch (start us, length us, event | category | flops | bytes accessed | tf_op | source)
XLA Modules:
  0.0 243.7 jit_solution(8984062820681312506)
XLA Ops:
  8.0 0.0 all-gather.3.cloned.1.call-start
  8.0 0.7 compare_select_fusion.2
  8.7 1.4 copy.106
  10.1 0.7 gather_fusion.1
  10.9 0.1 copy.107
  11.0 0.0 copy-start.1
  11.0 11.4 %all-gather = bf16[4,128,48]{1,2,0:T(8,128)(2,1)S(1)} all-gather(bf16[2,128,48]{1,2,0:T(8,128)(2,1)S(1)} %bitcast_convert_fusion), channel_id=2, replica_groups=mesh['dp_0'=2,'dp_1'=4,'dp_2'=8,'expert'=8] {'dp_0'}, dimensions={0}, use_global_device_ids=true | all-gather | bytes 73728 | tf_op jit(solution)/shard_map/all_gather | solution.py:33
  22.4 10.7 %all_gather.10 = bf16[8,2,128,48]{2,3,1,0:T(8,128)(2,1)} all-gather(bf16[2,2,128,48]{2,3,1,0:T(8,128)(2,1)S(1)} %bitcast.71), channel_id=1, replica_groups=mesh['dp_0'=2,'dp_1'=4,'dp_2'=8,'expert'=8] {'dp_1'}, dimensions={0}, use_global_device_ids=true | all-gather | bytes 245760 | tf_op jit(solution)/shard_map/all_gather | solution.py:33
  33.2 0.0 all-gather.3.cloned.1.call-update
  33.2 1.3 broadcast_in_dim.42
  34.5 9.8 %all-to-all-start = ((s32[8,1,1024]{2,1,0:T(1,128)}), s32[8,1,1024]{2,1,0:T(1,128)}, u32[]{:S(2)}, u32[]{:S(2)}) async-start(s32[8,1,1024]{2,1,0:T(1,128)} %broadcast_in_dim.42), calls=%async_computation | async-start | bytes 65536 | tf_op jit(solution)/shard_map/all_to_all | solution.py:23
  44.3 1.1 copy.108
  46.0 29.6 %all-gather.3.cloned.1.call-done = bf16[64,2,128,48]{2,3,1,0:T(8,128)(2,1)} async-done(((bf16[8,2,128,48]{2,3,1,0:T(8,128)(2,1)}), bf16[64,2,128,48]{2,3,1,0:T(8,128)(2,1)}) %all-gather.3.cloned.1.call-update) | async-done | bytes 1572880 | tf_op jit(solution)/shard_map/all_gather | solution.py:33
  75.6 0.0 copy-done.1
  75.6 0.0 copy-start
  75.6 1.7 copy.109
  77.3 0.1 fusion.25
  77.5 1.4 copy-done
  78.9 2.2 fusion
  81.1 3.8 %fusion.10 = f32[128,3072]{0,1:T(8,128)} fusion(bf16[1024,3072]{1,0:T(8,128)(2,1)S(1)} %copy-done, f32[1024,128]{0,1:T(8,128)S(1)} %fusion, bf16[1024,128]{0,1:T(8,128)(2,1)S(1)} %copy.108, f32[1024]{0:T(1024)S(1)} %fusion.18), kind=kOutput, calls=%fused_computation.21 | convolution fusion | flops 806354944 | bytes 8654848 | tf_op jit(solution)/shard_map/stack | solution.py:125
  84.9 9.7 %fusion.6 = f32[128,3072]{0,1:T(8,128)} fusion(bf16[1024,3072]{1,0:T(8,128)(2,1)} %param.9, bf16[128,3072]{0,1:T(8,128)(2,1)S(1)} %bitcast.68, f32[1024,128]{0,1:T(8,128)S(1)} %fusion, bf16[1024,128]{0,1:T(8,128)(2,1)S(1)} %copy.108, f32[1024]{0:T(1024)S(1)} %fusion.18), kind=kOutput, calls=%fused_computation.13 | convolution fusion | flops 1612316672 | bytes 9441280 | tf_op jit(solution)/shard_map/stack | solution.py:125
  94.6 2.2 maximum_multiply_fusion
  96.8 2.1 copy.112
  98.9 0.0 copy-start.6
  98.9 0.0 copy-start.3
  98.9 0.0 all-to-all-done
  98.9 6.7 %all-to-all-start.2 = ((f32[32,2,2,128,48]{3,4,2,1,0:T(8,128)}), f32[32,2,2,128,48]{3,4,2,1,0:T(8,128)S(1)}, u32[]{:S(2)}, u32[]{:S(2)}) async-start(f32[32,2,2,128,48]{3,4,2,1,0:T(8,128)} %copy.112), calls=%async_computation.2 | async-start | bytes 6291456 | tf_op jit(solution)/shard_map/all_to_all | solution.py:51
  105.6 0.0 sort.32.cloned.1.call-start
  105.6 0.0 copy-done.6
  105.6 1.5 iota_select_fusion
  107.1 0.6 broadcast_in_dim.44
  107.7 0.0 sort.32.cloned.1.call-update
  107.7 0.0 copy-done.3
  107.8 1.3 copy.102
  109.0 5.8 %sort.32.cloned.1.call-done = (s32[8,1024]{1,0:T(8,128)}, s32[8,1024]{1,0:T(8,128)}) async-done(((s32[8,1024]{1,0:T(8,128)}, s32[8,1024]{1,0:T(8,128)}), (s32[8,1024]{1,0:T(8,128)}, s32[8,1024]{1,0:T(8,128)})) %sort.32.cloned.1.call-update) | async-done | bytes 65552 | tf_op jit(solution)/shard_map/vmap(jit(argsort))/sort | solution.py:77
  114.8 0.7 slice.15
  115.5 8.8 %gather_fusion = f32[1024,2,48]{2,1,0:T(2,128)} fusion(f32[2,1024,48]{2,0,1:T(2,128)} %copy.102, s32[1024]{0:T(1024)S(1)} %broadcast_clamp_fusion), kind=kCustom, calls=%fused_computation | custom fusion | bytes 790528 | tf_op jit(solution)/shard_map/gather | solution.py:90
  124.3 2.1 copy.103
  126.4 48.7 %all-to-all-done.2 = f32[32,2,2,128,48]{3,4,2,1,0:T(8,128)S(1)} async-done(((f32[32,2,2,128,48]{3,4,2,1,0:T(8,128)}), f32[32,2,2,128,48]{3,4,2,1,0:T(8,128)S(1)}, u32[]{:S(2)}, u32[]{:S(2)}) %all-to-all-start.2) | async-done | bytes 3145760 | tf_op jit(solution)/shard_map/all_to_all | solution.py:51
  175.0 10.7 %all-to-all-start.1 = ((f32[2,8,128,48]{2,3,0,1:T(8,128)}), f32[2,8,128,48]{2,3,0,1:T(8,128)S(1)}, u32[]{:S(2)}, u32[]{:S(2)}) async-start(f32[2,8,128,48]{2,3,0,1:T(8,128)} %copy.103), calls=%async_computation.1 | async-start | bytes 786432 | tf_op jit(solution)/shard_map/all_to_all | solution.py:93
  185.8 0.0 sort.30.cloned.1.call-start
  185.8 0.6 broadcast_in_dim.41
  186.4 0.0 sort.30.cloned.1.call-update
  186.4 8.6 %sort.30.cloned.1.call-done = (s32[8,1024]{1,0:T(8,128)}, s32[8,1024]{1,0:T(8,128)}) async-done(((s32[8,1024]{1,0:T(8,128)}, s32[8,1024]{1,0:T(8,128)}), (s32[8,1024]{1,0:T(8,128)}, s32[8,1024]{1,0:T(8,128)})) %sort.30.cloned.1.call-update) | async-done | bytes 65552 | tf_op jit(solution)/shard_map/vmap(jit(argsort))/sort | solution.py:77
  195.0 0.7 slice.14
  195.7 0.8 reduce_sum.18
  196.5 0.6 all-to-all-done.1
  197.1 5.4 %all-to-all-start.3 = ((f32[2,2,128,48]{2,3,1,0:T(8,128)}), f32[2,2,128,48]{2,3,1,0:T(8,128)S(1)}, u32[]{:S(2)}, u32[]{:S(2)}) async-start(f32[2,2,128,48]{2,3,1,0:T(8,128)} %reduce_sum.18), calls=%async_computation.3 | async-start | bytes 196608 | tf_op jit(solution)/shard_map/all_to_all | solution.py:58
  202.5 0.0 copy-start.2
  202.5 0.0 copy-start.4
  202.5 0.0 copy-start.5
  202.5 0.6 copy.105
  203.1 0.3 broadcast_in_dim.38
  203.4 26.6 %scatter_fusion = f32[2,1024,48]{2,0,1:T(2,128)S(1)} fusion(f32[2,1024,48]{2,0,1:T(2,128)S(1)} %broadcast_in_dim.38, s32[1024]{0:T(1024)S(1)} %bitcast.72, f32[1024,2,48]{2,1,0:T(2,128)S(1)} %copy.105), kind=kCustom, calls=%fused_computation.2 | custom fusion | bytes 1183744 | tf_op jit(solution)/shard_map/scatter | solution.py:100
  230.0 0.0 all-to-all-done.3
  230.0 0.0 copy-done.2
  230.0 0.0 copy-done.4
  230.0 0.0 copy-done.5
  230.0 0.7 fusion.17
  230.7 0.1 copy.114
  230.8 4.3 %scatter_fusion.1 = f32[2,1024,48]{2,0,1:T(2,128)S(1)} fusion(f32[2,1024,48]{2,0,1:T(2,128)S(1)} %scatter_fusion, s32[128]{0:T(128)S(1)} %compare_select_fusion.2, f32[128,2,48]{2,1,0:T(2,128)S(1)} %copy.114), kind=kCustom, calls=%fused_computation.3 | custom fusion | bytes 147968 | tf_op jit(solution)/shard_map/scatter | solution.py:132
  235.1 1.1 copy.115
  (10 shorter events, 0.1 us)
Async XLA Ops:
  8.0 67.6 %all-gather.3.cloned.1.call-start = ((), (), s32[]{:S(2)}) async-start(), calls=%async_computation.4 | async-start | bytes 1769472 | tf_op jit(solution)/shard_map/all_gather | solution.py:33
  11.0 64.7 %copy-start.1 = (f32[128,2,48]{0,2,1:T(8,128)}, f32[128,2,48]{0,2,1:T(8,128)S(1)}, u32[]{:S(2)}) copy-start(f32[128,2,48]{0,2,1:T(8,128)S(1)} %copy.107) | copy-start | bytes 147460
  34.5 64.4 %all-to-all-start = ((s32[8,1,1024]{2,1,0:T(1,128)}), s32[8,1,1024]{2,1,0:T(1,128)}, u32[]{:S(2)}, u32[]{:S(2)}) async-start(s32[8,1,1024]{2,1,0:T(1,128)} %broadcast_in_dim.42), calls=%async_computation | async-start | bytes 65536 | tf_op jit(solution)/shard_map/all_to_all | solution.py:23
  75.6 3.3 %copy-start = (bf16[1024,3072]{1,0:T(8,128)(2,1)S(1)}, bf16[1024,3072]{1,0:T(8,128)(2,1)}, u32[]{:S(2)}) copy-start(bf16[1024,3072]{1,0:T(8,128)(2,1)} %param.9) | copy-start | bytes 18874372
  98.9 6.8 %copy-start.6 = (s32[1024]{0:T(1024)S(1)}, s32[1024]{0:T(1024)}, u32[]{:S(2)}) copy-start(s32[1024]{0:T(1024)} %param.17) | copy-start | bytes 12292
  98.9 8.9 %copy-start.3 = (f32[2,1024,48]{1,2,0:T(8,128)S(1)}, f32[2,1024,48]{1,2,0:T(8,128)}, u32[]{:S(2)}) copy-start(f32[2,1024,48]{1,2,0:T(8,128)} %param.16) | copy-start | bytes 1179652
  98.9 76.2 %all-to-all-start.2 = ((f32[32,2,2,128,48]{3,4,2,1,0:T(8,128)}), f32[32,2,2,128,48]{3,4,2,1,0:T(8,128)S(1)}, u32[]{:S(2)}, u32[]{:S(2)}) async-start(f32[32,2,2,128,48]{3,4,2,1,0:T(8,128)} %copy.112), calls=%async_computation.2 | async-start | bytes 6291456 | tf_op jit(solution)/shard_map/all_to_all | solution.py:51
  105.6 9.3 %sort.32.cloned.1.call-start = ((), (), s32[]{:S(2)}) async-start(), calls=%async_computation.6 | async-start | bytes 196640 | tf_op jit(solution)/shard_map/vmap(jit(argsort))/sort | solution.py:77
  175.0 22.1 %all-to-all-start.1 = ((f32[2,8,128,48]{2,3,0,1:T(8,128)}), f32[2,8,128,48]{2,3,0,1:T(8,128)S(1)}, u32[]{:S(2)}, u32[]{:S(2)}) async-start(f32[2,8,128,48]{2,3,0,1:T(8,128)} %copy.103), calls=%async_computation.1 | async-start | bytes 786432 | tf_op jit(solution)/shard_map/all_to_all | solution.py:93
  185.8 9.3 %sort.30.cloned.1.call-start = ((), (), s32[]{:S(2)}) async-start(), calls=%async_computation.5 | async-start | bytes 196640 | tf_op jit(solution)/shard_map/vmap(jit(argsort))/sort | solution.py:77
  197.1 32.9 %all-to-all-start.3 = ((f32[2,2,128,48]{2,3,1,0:T(8,128)}), f32[2,2,128,48]{2,3,1,0:T(8,128)S(1)}, u32[]{:S(2)}, u32[]{:S(2)}) async-start(f32[2,2,128,48]{2,3,1,0:T(8,128)} %reduce_sum.18), calls=%async_computation.3 | async-start | bytes 196608 | tf_op jit(solution)/shard_map/all_to_all | solution.py:58
  202.5 27.5 %copy-start.2 = (f32[128,2,48]{0,2,1:T(8,128)S(1)}, f32[128,2,48]{0,2,1:T(8,128)}, u32[]{:S(2)}) copy-start(f32[128,2,48]{0,2,1:T(8,128)} %copy-done.1) | copy-start | bytes 147460
  202.5 27.5 %copy-start.4 = (f32[2,128,48]{1,2,0:T(8,128)S(1)}, f32[2,128,48]{1,2,0:T(8,128)}, u32[]{:S(2)}) copy-start(f32[2,128,48]{1,2,0:T(8,128)} %param.13) | copy-start | bytes 147460
  202.5 27.5 %copy-start.5 = (f32[2,128,48]{1,2,0:T(8,128)S(1)}, f32[2,128,48]{1,2,0:T(8,128)}, u32[]{:S(2)}) copy-start(f32[2,128,48]{1,2,0:T(8,128)} %param.14) | copy-start | bytes 147460
Sparse Core Ops, SparseCore 0:
  33.3 42.2 all-gather.2
Sparse Core Ops, SparseCore 1:
  109.1 5.4 sort.36.cloned.1.call-done
  189.3 5.4 sort.34.cloned.1.call-done
  (2 shorter events, 0.0 us)
where the time goes:
time: 245 us; the launch traced here: 244 us
  waiting for transfers between devices  78.9 us (32%)
  local copies, waits for them, and re-layouts  72.2 us (29%)
  starting transfers between devices  32.6 us (13%)
  blocking collectives  22.2 us (9%)
  between operations  16.3 us (7%)
  matrix products  15.7 us (6%)
  other arithmetic  5.79 us (2%)
    all_to_all x1, waiting for transfers between devices, sum_at_owner(): lax.all_to_all(tiles, axis, split_axis=0, concat_axis=0, tiled=True)  48.7 us
    all_gather x1, waiting for transfers between devices, stacked_from(): tiles = lax.all_gather(tiles, axes[k], axis=0, tiled=True)  29.6 us
    scatter x1, local copies, waits for them, and re-layouts, return_cold(): received = jnp.zeros_like(cold_blocks).at[:, take_rows.reshape(-1), :].se...  26.6 us
    all_gather x2, blocking collectives, stacked_from(): tiles = lax.all_gather(tiles, axes[k], axis=0, tiled=True)  22.2 us
    sort x4, local copies, waits for them, and re-layouts, rows_with(): return jnp.argsort(sort_key, stable=True)[:capacity]  14.5 us
    another operation x2, matrix products, per_device(): jnp.stack([contract_first(d_gate, tokens), contract_first(d_up, tokens)])  13.5 us
    all_to_all x1, starting transfers between devices, return_cold(): lax.all_to_all(packed, 'expert', split_axis=1, concat_axis=1, tiled=True)  10.7 us
    all_to_all x1, starting transfers between devices, sent_to_all(): return lax.all_to_all(copies, axis, split_axis=0, concat_axis=0, tiled=True)  9.76 us
  transfers between devices with their start and end apart: 5, of which 3 were waited for; matrix products, arithmetic and copies ran while one was open for 28% of the time, Pallas kernels for 0%

commit v1 on v0

--- a/solution.py
+++ b/solution.py
@@ -30,7 +30,10 @@
 def stacked_from(value, axes, order):
     tiles = value[None]
     for k in order:
-        tiles = lax.all_gather(tiles, axes[k], axis=0, tiled=True)
+        devices = lax.axis_size(axes[k])
+        shards = jnp.stack([tiles for _ in range(devices)])
+        shards = lax.all_to_all(shards, axes[k], split_axis=0, concat_axis=0)
+        tiles = jnp.concatenate(shards, axis=0)
     block = [lax.axis_size(axes[k]) for k in reversed(order)]
     tiles = tiles.reshape(*block, *value.shape)
     turned = sorted(range(len(order)), key=lambda place: order[len(order) - 1 - place])

time: 245 us -> 254 us (1.037)
  waiting for transfers between devices: 78.9 us -> 88.4 us
  blocking collectives: 22.2 us -> 26.6 us
  starting transfers between devices: 32.6 us -> 29.6 us
    all_to_all x0 -> x1, waiting for transfers between devices: none -> 36.9 us  [stacked_from(): shards = lax.all_to_all(shards, axes[k], split_axis=0, concat_axis=0)]
    all_gather x1 -> x0, waiting for transfers between devices: 29.6 us -> none  [stacked_from(): tiles = lax.all_gather(tiles, axes[k], axis=0, tiled=True)]
    all_to_all x0 -> x2, blocking collectives: none -> 26.6 us  [stacked_from(): shards = lax.all_to_all(shards, axes[k], split_axis=0, concat_axis=0)]
    all_gather x2 -> x0, blocking collectives: 22.2 us -> none  [stacked_from(): tiles = lax.all_gather(tiles, axes[k], axis=0, tiled=True)]
    all_to_all x0 -> x1, starting transfers between devices: none -> 6.82 us  [stacked_from(): shards = lax.all_to_all(shards, axes[k], split_axis=0, concat_axis=0)]
    all_to_all x1, starting transfers between devices: 10.7 us -> 7.8 us  [return_cold(): lax.all_to_all(packed, 'expert', split_axis=1, concat_axis=1, tiled=True)]
    all_to_all x1, waiting for transfers between devices: 48.7 us -> 51.3 us  [sum_at_owner(): lax.all_to_all(tiles, axis, split_axis=0, concat_axis=0, tiled=True)]
    unnamed x20 -> x22, local copies, waits for them, and re-layouts: 6.4 us -> 6.65 us
  transfers between devices with their start and end apart: 5 -> 5, of which waited for: 3 -> 3; matrix products, arithmetic and copies ran while one was open for 28% -> 26% of each run, Pallas kernels for 0% -> 0%
where the time goes in v1:
time: 254 us; the launch traced here: 253 us
  waiting for transfers between devices  88.4 us (35%)
  local copies, waits for them, and re-layouts  72.3 us (28%)
  starting transfers between devices  29.6 us (12%)
  blocking collectives  26.6 us (10%)
  matrix products  15.7 us (6%)
  between operations  14.9 us (6%)
  other arithmetic  5.8 us (2%)
    all_to_all x1, waiting for transfers between devices, sum_at_owner(): lax.all_to_all(tiles, axis, split_axis=0, concat_axis=0, tiled=True)  51.3 us
    all_to_all x1, waiting for transfers between devices, stacked_from(): shards = lax.all_to_all(shards, axes[k], split_axis=0, concat_axis=0)  36.9 us
    all_to_all x2, blocking collectives, stacked_from(): shards = lax.all_to_all(shards, axes[k], split_axis=0, concat_axis=0)  26.6 us
    scatter x1, local copies, waits for them, and re-layouts, return_cold(): received = jnp.zeros_like(cold_blocks).at[:, take_rows.reshape(-1), :].se...  26.6 us
    sort x4, local copies, waits for them, and re-layouts, rows_with(): return jnp.argsort(sort_key, stable=True)[:capacity]  15.1 us
    another operation x2, matrix products, per_device(): jnp.stack([contract_first(d_gate, tokens), contract_first(d_up, tokens)])  13.5 us
    gather x1, local copies, waits for them, and re-layouts, return_cold(): cold_blocks[:, send_rows.reshape(-1), :]  8.77 us
    all_to_all x1, starting transfers between devices, return_cold(): lax.all_to_all(packed, 'expert', split_axis=1, concat_axis=1, tiled=True)  7.8 us
  transfers between devices with their start and end apart: 5, of which 3 were waited for; matrix products, arithmetic and copies ran while one was open for 26% of the time, Pallas kernels for 0%

profile of v1, /device:TPU:1, one launch (start us, length us, event | category | flops | bytes accessed | tf_op | source)
XLA Modules:
  0.0 253.5 jit_solution(6226526137532996484)
XLA Ops:
  7.2 0.7 compare_select_fusion.2
  7.8 1.4 copy.111
  9.3 0.0 copy-start.4
  9.3 0.7 gather_fusion.1
  10.0 0.1 copy.112
  10.1 0.0 copy-start.1
  10.1 0.0 copy-start.7
  10.2 17.6 %all_to_all.39 = bf16[2,1,2,128,48]{3,4,2,1,0:T(8,128)(2,1)S(1)} all-to-all(bf16[2,1,2,128,48]{3,4,2,1,0:T(8,128)(2,1)S(1)} %pad_maximum_fusion), channel_id=1, replica_groups=mesh['dp_0'=2,'dp_1'=4,'dp_2'=8,'expert'=8] {'dp_0'}, dimensions={0} | all-to-all | bytes 98304 | tf_op jit(solution)/shard_map/all_to_all | solution.py:35
  27.8 0.0 copy-done.1
  27.8 9.0 %all_to_all.40 = bf16[4,2,2,128,48]{3,4,2,1,0:T(8,128)(2,1)S(1)} all-to-all(bf16[4,2,2,128,48]{3,4,2,1,0:T(8,128)(2,1)S(1)} %stack.19), channel_id=1, replica_groups=mesh['dp_0'=2,'dp_1'=4,'dp_2'=8,'expert'=8] {'dp_1'}, dimensions={0} | all-to-all | bytes 393216 | tf_op jit(solution)/shard_map/all_to_all | solution.py:35
  36.8 1.4 stack.20
  38.2 6.8 %all-to-all-start.4 = ((bf16[8,8,2,128,48]{3,4,2,1,0:T(8,128)(2,1)}), bf16[8,8,2,128,48]{3,4,2,1,0:T(8,128)(2,1)S(1)}, u32[]{:S(2)}, u32[]{:S(2)}) async-start(bf16[8,8,2,128,48]{3,4,2,1,0:T(8,128)(2,1)} %stack.20), calls=%async_computation.4 | async-start | bytes 3145728 | tf_op jit(solution)/shard_map/all_to_all | solution.py:35
  45.1 0.0 copy-done.4
  45.1 0.1 copy.113
  45.9 36.9 %all-to-all-done.4 = bf16[8,8,2,128,48]{3,4,2,1,0:T(8,128)(2,1)S(1)} async-done(((bf16[8,8,2,128,48]{3,4,2,1,0:T(8,128)(2,1)}), bf16[8,8,2,128,48]{3,4,2,1,0:T(8,128)(2,1)S(1)}, u32[]{:S(2)}, u32[]{:S(2)}) %all-to-all-start.4) | async-done | bytes 1572896 | tf_op jit(solution)/shard_map/all_to_all | solution.py:35
  82.8 0.0 copy-done.7
  82.8 0.6 broadcast_in_dim.41
  83.5 7.5 %all-to-all-start = ((s32[8,1,1024]{2,1,0:T(1,128)}), s32[8,1,1024]{2,1,0:T(1,128)}, u32[]{:S(2)}, u32[]{:S(2)}) async-start(s32[8,1,1024]{2,1,0:T(1,128)} %broadcast_in_dim.41), calls=%async_computation | async-start | bytes 65536 | tf_op jit(solution)/shard_map/all_to_all | solution.py:23
  91.0 0.0 copy-start
  91.0 0.1 copy.114
  91.1 0.1 fusion.26
  91.2 2.5 copy-done
  93.7 2.2 fusion
  95.9 3.8 %fusion.10 = f32[128,3072]{0,1:T(8,128)} fusion(bf16[1024,3072]{1,0:T(8,128)(2,1)S(1)} %copy-done, f32[1024,128]{0,1:T(8,128)S(1)} %fusion, bf16[1024,128]{0,1:T(8,128)(2,1)S(1)} %copy.113, f32[1024]{0:T(1024)S(1)} %fusion.19), kind=kOutput, calls=%fused_computation.21 | convolution fusion | flops 806354944 | bytes 8654848 | tf_op jit(solution)/shard_map/stack | solution.py:128
  99.8 9.7 %fusion.6 = f32[128,3072]{0,1:T(8,128)} fusion(bf16[1024,3072]{1,0:T(8,128)(2,1)} %param.9, bf16[128,3072]{0,1:T(8,128)(2,1)S(1)} %bitcast.74, f32[1024,128]{0,1:T(8,128)S(1)} %fusion, bf16[1024,128]{0,1:T(8,128)(2,1)S(1)} %copy.113, f32[1024]{0:T(1024)S(1)} %fusion.19), kind=kOutput, calls=%fused_computation.13 | convolution fusion | flops 1612316672 | bytes 9441280 | tf_op jit(solution)/shard_map/stack | solution.py:128
  109.4 2.2 maximum_multiply_fusion
  111.6 2.1 copy.117
  113.7 0.0 copy-start.3
  113.7 0.0 all-to-all-done
  113.7 4.2 %all-to-all-start.5 = ((f32[32,2,2,128,48]{3,4,2,1,0:T(8,128)}), f32[32,2,2,128,48]{3,4,2,1,0:T(8,128)S(1)}, u32[]{:S(2)}, u32[]{:S(2)}) async-start(f32[32,2,2,128,48]{3,4,2,1,0:T(8,128)} %copy.117), calls=%async_computation.5 | async-start | bytes 6291456 | tf_op jit(solution)/shard_map/all_to_all | solution.py:54
  117.9 0.0 sort.32.cloned.1.call-start
  118.0 1.5 iota_select_fusion
  119.4 0.6 broadcast_in_dim.43
  120.0 0.0 sort.32.cloned.1.call-update
  120.1 0.0 copy-done.3
  120.1 1.3 copy.107
  121.3 6.2 %sort.32.cloned.1.call-done = (s32[8,1024]{1,0:T(8,128)}, s32[8,1024]{1,0:T(8,128)}) async-done(((s32[8,1024]{1,0:T(8,128)}, s32[8,1024]{1,0:T(8,128)}), (s32[8,1024]{1,0:T(8,128)}, s32[8,1024]{1,0:T(8,128)})) %sort.32.cloned.1.call-update) | async-done | bytes 65552 | tf_op jit(solution)/shard_map/vmap(jit(argsort))/sort | solution.py:80
  127.5 0.7 slice.15
  128.2 8.8 %gather_fusion = f32[1024,2,48]{2,1,0:T(2,128)} fusion(f32[2,1024,48]{2,0,1:T(2,128)} %copy.107, s32[1024]{0:T(1024)S(1)} %broadcast_clamp_fusion), kind=kCustom, calls=%fused_computation | custom fusion | bytes 790528 | tf_op jit(solution)/shard_map/gather | solution.py:93
  137.0 2.1 copy.108
  139.1 51.3 %all-to-all-done.5 = f32[32,2,2,128,48]{3,4,2,1,0:T(8,128)S(1)} async-done(((f32[32,2,2,128,48]{3,4,2,1,0:T(8,128)}), f32[32,2,2,128,48]{3,4,2,1,0:T(8,128)S(1)}, u32[]{:S(2)}, u32[]{:S(2)}) %all-to-all-start.5) | async-done | bytes 3145760 | tf_op jit(solution)/shard_map/all_to_all | solution.py:54
  190.4 7.8 %all-to-all-start.1 = ((f32[2,8,128,48]{2,3,0,1:T(8,128)}), f32[2,8,128,48]{2,3,0,1:T(8,128)S(1)}, u32[]{:S(2)}, u32[]{:S(2)}) async-start(f32[2,8,128,48]{2,3,0,1:T(8,128)} %copy.108), calls=%async_computation.1 | async-start | bytes 786432 | tf_op jit(solution)/shard_map/all_to_all | solution.py:96
  198.2 0.0 sort.30.cloned.1.call-start
  198.2 0.6 broadcast_in_dim.40
  198.8 0.1 sort.30.cloned.1.call-update
  198.9 8.9 %sort.30.cloned.1.call-done = (s32[8,1024]{1,0:T(8,128)}, s32[8,1024]{1,0:T(8,128)}) async-done(((s32[8,1024]{1,0:T(8,128)}, s32[8,1024]{1,0:T(8,128)}), (s32[8,1024]{1,0:T(8,128)}, s32[8,1024]{1,0:T(8,128)})) %sort.30.cloned.1.call-update) | async-done | bytes 65552 | tf_op jit(solution)/shard_map/vmap(jit(argsort))/sort | solution.py:80
  207.8 0.7 slice.14
  208.5 0.8 reduce_sum.18
  209.3 0.2 all-to-all-done.1
  209.5 3.3 %all-to-all-start.6 = ((f32[2,2,128,48]{2,3,1,0:T(8,128)}), f32[2,2,128,48]{2,3,1,0:T(8,128)S(1)}, u32[]{:S(2)}, u32[]{:S(2)}) async-start(f32[2,2,128,48]{2,3,1,0:T(8,128)} %reduce_sum.18), calls=%async_computation.6 | async-start | bytes 196608 | tf_op jit(solution)/shard_map/all_to_all | solution.py:61
  212.8 0.0 copy-start.2
  212.8 0.0 copy-start.5
  212.8 0.0 copy-start.6
  212.9 0.6 copy.110
  213.4 0.3 broadcast_in_dim.37
  213.7 26.6 %scatter_fusion = f32[2,1024,48]{2,0,1:T(2,128)S(1)} fusion(f32[2,1024,48]{2,0,1:T(2,128)S(1)} %broadcast_in_dim.37, s32[1024]{0:T(1024)S(1)} %bitcast.78, f32[1024,2,48]{2,1,0:T(2,128)S(1)} %copy.110), kind=kCustom, calls=%fused_computation.2 | custom fusion | bytes 1183744 | tf_op jit(solution)/shard_map/scatter | solution.py:103
  240.3 0.0 all-to-all-done.6
  240.4 0.0 copy-done.2
  240.4 0.0 copy-done.5
  240.4 0.0 copy-done.6
  240.4 0.7 fusion.17
  241.0 0.1 copy.119
  241.2 4.3 %scatter_fusion.1 = f32[2,1024,48]{2,0,1:T(2,128)S(1)} fusion(f32[2,1024,48]{2,0,1:T(2,128)S(1)} %scatter_fusion, s32[128]{0:T(128)S(1)} %compare_select_fusion.2, f32[128,2,48]{2,1,0:T(2,128)S(1)} %copy.119), kind=kCustom, calls=%fused_computation.3 | custom fusion | bytes 147968 | tf_op jit(solution)/shard_map/scatter | solution.py:135
  245.5 1.1 copy.120
  (12 shorter events, 0.1 us)
Async XLA Ops:
  9.3 35.8 %copy-start.4 = (bf16[1024,128]{1,0:T(8,128)(2,1)S(1)}, bf16[1024,128]{1,0:T(8,128)(2,1)}, u32[]{:S(2)}) copy-start(bf16[1024,128]{1,0:T(8,128)(2,1)} %param.10) | copy-start | bytes 786436
  10.1 17.7 %copy-start.1 = (f32[128,2,48]{0,2,1:T(8,128)}, f32[128,2,48]{0,2,1:T(8,128)S(1)}, u32[]{:S(2)}) copy-start(f32[128,2,48]{0,2,1:T(8,128)S(1)} %copy.112) | copy-start | bytes 147460
  10.1 72.7 %copy-start.7 = (s32[1024]{0:T(1024)S(1)}, s32[1024]{0:T(1024)}, u32[]{:S(2)}) copy-start(s32[1024]{0:T(1024)} %param.17) | copy-start | bytes 12292
  38.2 44.6 %all-to-all-start.4 = ((bf16[8,8,2,128,48]{3,4,2,1,0:T(8,128)(2,1)}), bf16[8,8,2,128,48]{3,4,2,1,0:T(8,128)(2,1)S(1)}, u32[]{:S(2)}, u32[]{:S(2)}) async-start(bf16[8,8,2,128,48]{3,4,2,1,0:T(8,128)(2,1)} %stack.20), calls=%async_computation.4 | async-start | bytes 3145728 | tf_op jit(solution)/shard_map/all_to_all | solution.py:35
  83.5 30.2 %all-to-all-start = ((s32[8,1,1024]{2,1,0:T(1,128)}), s32[8,1,1024]{2,1,0:T(1,128)}, u32[]{:S(2)}, u32[]{:S(2)}) async-start(s32[8,1,1024]{2,1,0:T(1,128)} %broadcast_in_dim.41), calls=%async_computation | async-start | bytes 65536 | tf_op jit(solution)/shard_map/all_to_all | solution.py:23
  91.0 2.8 %copy-start = (bf16[1024,3072]{1,0:T(8,128)(2,1)S(1)}, bf16[1024,3072]{1,0:T(8,128)(2,1)}, u32[]{:S(2)}) copy-start(bf16[1024,3072]{1,0:T(8,128)(2,1)} %param.9) | copy-start | bytes 18874372
  113.7 6.4 %copy-start.3 = (f32[2,1024,48]{1,2,0:T(8,128)S(1)}, f32[2,1024,48]{1,2,0:T(8,128)}, u32[]{:S(2)}) copy-start(f32[2,1024,48]{1,2,0:T(8,128)} %param.16) | copy-start | bytes 1179652
  113.7 76.7 %all-to-all-start.5 = ((f32[32,2,2,128,48]{3,4,2,1,0:T(8,128)}), f32[32,2,2,128,48]{3,4,2,1,0:T(8,128)S(1)}, u32[]{:S(2)}, u32[]{:S(2)}) async-start(f32[32,2,2,128,48]{3,4,2,1,0:T(8,128)} %copy.117), calls=%async_computation.5 | async-start | bytes 6291456 | tf_op jit(solution)/shard_map/all_to_all | solution.py:54
  117.9 9.7 %sort.32.cloned.1.call-start = ((), (), s32[]{:S(2)}) async-start(), calls=%async_computation.8 | async-start | bytes 196640 | tf_op jit(solution)/shard_map/vmap(jit(argsort))/sort | solution.py:80
  190.4 19.1 %all-to-all-start.1 = ((f32[2,8,128,48]{2,3,0,1:T(8,128)}), f32[2,8,128,48]{2,3,0,1:T(8,128)S(1)}, u32[]{:S(2)}, u32[]{:S(2)}) async-start(f32[2,8,128,48]{2,3,0,1:T(8,128)} %copy.108), calls=%async_computation.1 | async-start | bytes 786432 | tf_op jit(solution)/shard_map/all_to_all | solution.py:96
  198.2 9.6 %sort.30.cloned.1.call-start = ((), (), s32[]{:S(2)}) async-start(), calls=%async_computation.7 | async-start | bytes 196640 | tf_op jit(solution)/shard_map/vmap(jit(argsort))/sort | solution.py:80
  209.5 30.9 %all-to-all-start.6 = ((f32[2,2,128,48]{2,3,1,0:T(8,128)}), f32[2,2,128,48]{2,3,1,0:T(8,128)S(1)}, u32[]{:S(2)}, u32[]{:S(2)}) async-start(f32[2,2,128,48]{2,3,1,0:T(8,128)} %reduce_sum.18), calls=%async_computation.6 | async-start | bytes 196608 | tf_op jit(solution)/shard_map/all_to_all | solution.py:61
  212.8 27.5 %copy-start.2 = (f32[128,2,48]{0,2,1:T(8,128)S(1)}, f32[128,2,48]{0,2,1:T(8,128)}, u32[]{:S(2)}) copy-start(f32[128,2,48]{0,2,1:T(8,128)} %copy-done.1) | copy-start | bytes 147460
  212.8 27.5 %copy-start.5 = (f32[2,128,48]{1,2,0:T(8,128)S(1)}, f32[2,128,48]{1,2,0:T(8,128)}, u32[]{:S(2)}) copy-start(f32[2,128,48]{1,2,0:T(8,128)} %param.13) | copy-start | bytes 147460
  212.8 27.5 %copy-start.6 = (f32[2,128,48]{1,2,0:T(8,128)S(1)}, f32[2,128,48]{1,2,0:T(8,128)}, u32[]{:S(2)}) copy-start(f32[2,128,48]{1,2,0:T(8,128)} %param.14) | copy-start | bytes 147460
Sparse Core Ops, SparseCore 0:
  121.7 5.5 sort.36.cloned.1.call-done
  202.0 5.4 sort.34.cloned.1.call-done
  (2 shorter events, 0.0 us)
